TPU v7x, 1024 devices: a whole 4x4x32 slice. The times are simulated.
1024 devices in a mesh: dp: 32 (over y, x, core), expert: 32 (over z).
Axes of the slice: x: 4, y: 4, z: 32, core: 2. Of those that a mesh axis runs over, the one named last changes fastest.
Arguments:
- tokens: bfloat16 [131072, 2048], P(('dp', 'expert')), may hold values from -6 to 6
- out_grad: bfloat16 [131072, 2048], P(('dp', 'expert')), may hold values from -6 to 6
- gate_prob: float32 [131072, 1], P(('dp', 'expert')), may hold values from 0.2 to 1
- routing: int32 [131072, 1], P(('dp', 'expert')), may hold values from 0 to 31; in each aligned block of 128 rows (0 to 127, 128 to 255, ...) at most 8 rows name the same one
- expert_weights: bfloat16 [32, 2048, 1152], P('expert'), may hold values from -0.125 to 0.125
Outputs:
- input_grad: bfloat16 [131072, 2048], P(('dp', 'expert'))
- weight_grad: float32 [32, 2048, 1152], P('expert', 'dp')
Inputs may be any that keep to these rules, and one draw needn't show every extreme that they name: `routing`: among the tokens of one device at most 8 go to any one expert; in some devices' tokens an expert gets exactly 8.
All inputs are finite; a program needn't handle non-finite values.
Results may differ from a plain program's by a relative error of at most 0.014.
Values may be sent and summed in bfloat16 or wider, within the bound.
A program may use at most 64 MiB of HBM per device.

v0:
```python
import jax
import jax.numpy as jnp
from jax import lax
from jax.sharding import Mesh
from jax.sharding import PartitionSpec as P

DP = ("dp_0", "dp_1", "dp_2")
DP_EXPERT = ("dp_0", "dp_1", "dp_2", "expert")


def in_blocks(value, dim, length):
    before, after = (value.shape[:dim], value.shape[dim + 1 :])
    return jnp.moveaxis(value.reshape(*before, length, -1, *after), dim, 0)


def scatter_pairs(value, chips, core, dim):
    sizes = (lax.axis_size(chips), lax.axis_size(core))
    parts = in_blocks(value, dim, sizes[0] * sizes[1])
    inside = parts.shape[1:]
    parts = parts.reshape(*sizes, *inside).swapaxes(0, 1).reshape(-1, *inside)
    parts = lax.psum_scatter(parts, core, scatter_dimension=0, tiled=True)
    return lax.psum_scatter(parts, chips, scatter_dimension=0, tiled=True)[0]


def side_by_side(arrays, axis, split_dim, concat_dim, along):
    widths = [a.shape[along] for a in arrays]
    both = jnp.concatenate(arrays, axis=along)
    filled = lax.all_to_all(both, axis, split_axis=split_dim, concat_axis=concat_dim, tiled=True)
    return tuple(jnp.split(filled, [sum(widths[:k]) for k in range(1, len(widths))], axis=along))


def slot_of(route_block, capacity, experts):
    onehot = (route_block[:, None] == jnp.arange(experts, dtype=jnp.int32)[None, :]).astype(
        jnp.int32
    )
    before = jnp.cumsum(onehot, axis=0) - onehot
    position = jnp.sum(before * onehot, axis=1)
    return route_block * capacity + position


def expert_rows(weights, rows_in, grad_in):
    hidden_width = weights.shape[1] // 3
    pair_weights = weights[:, : 2 * hidden_width]
    down_weights = weights[:, 2 * hidden_width :]
    pre_act = jnp.dot(rows_in, pair_weights, preferred_element_type=jnp.float32)
    pre_gate = pre_act[:, :hidden_width]
    pre_up = pre_act[:, hidden_width:]
    sigmoid_gate = jax.nn.sigmoid(pre_gate)
    active = pre_gate * sigmoid_gate
    hidden = (active * pre_up).astype(jnp.bfloat16)
    grad_hidden = jnp.dot(grad_in, down_weights, preferred_element_type=jnp.float32)
    grad_gate = grad_hidden * pre_up * (sigmoid_gate * (1.0 + pre_gate * (1.0 - sigmoid_gate)))
    grad_up = grad_hidden * active
    grad_pair = jnp.concatenate(
        [grad_gate.astype(jnp.bfloat16), grad_up.astype(jnp.bfloat16)], axis=1
    )
    returned = lax.dot_general(
        grad_pair, pair_weights, (((1,), (1,)), ((), ())), preferred_element_type=jnp.float32
    )
    return (returned.astype(jnp.bfloat16), hidden, grad_pair)


def weight_term(rows_in, grad_in, hidden, grad_pair, grad_scale):
    contract = (((0,), (0,)), ((), ()))
    first_part = lax.dot_general(rows_in, grad_pair, contract, preferred_element_type=jnp.float32)
    second = lax.dot_general(grad_in, hidden, contract, preferred_element_type=jnp.float32)
    return grad_scale * jnp.concatenate([first_part, second], axis=1)


def sum_weights(rows_in, grad_in, hidden, grad_pair, grad_scale):
    return scatter_pairs(
        weight_term(rows_in, grad_in, hidden, grad_pair, grad_scale).astype(jnp.bfloat16),
        ("dp_0", "dp_1"),
        "dp_2",
        0,
    ).astype(jnp.float32)


def send_back(returned):
    return lax.all_to_all(returned, "expert", split_axis=0, concat_axis=0, tiled=True)


def local(tokens, out_grad, gate_prob, routing, expert_weights):
    tok_dev, model_width = tokens.shape
    experts = lax.axis_size("expert")
    replicas = lax.axis_size(DP)
    capacity = 2 * tok_dev // experts
    share_rows = model_width // replicas
    grad_scale = float(tok_dev * replicas) ** (-0.5)
    weights = expert_weights[0]
    hidden_width = weights.shape[1] // 3
    scaled = (gate_prob * out_grad.astype(jnp.float32)).astype(jnp.bfloat16)
    slot_index = slot_of(routing[:, 0], capacity, experts)
    dispatch_table = (
        jnp.arange(experts * capacity, dtype=jnp.int32)[:, None] == slot_index[None, :]
    ).astype(jnp.bfloat16)
    send_x = (
        jnp.dot(dispatch_table, tokens, preferred_element_type=jnp.float32)
        .astype(jnp.bfloat16)
        .reshape(experts, capacity, model_width)
    )
    send_g = (
        jnp.dot(dispatch_table, scaled, preferred_element_type=jnp.float32)
        .astype(jnp.bfloat16)
        .reshape(experts, capacity, model_width)
    )
    recv_x, recv_g = side_by_side((send_x, send_g), "expert", 0, 0, 1)
    rows_in = recv_x.reshape(experts * capacity, model_width)
    grad_in = recv_g.reshape(experts * capacity, model_width)
    returned, hidden, grad_pair = expert_rows(weights, rows_in, grad_in)
    returned = returned.reshape(experts, capacity, model_width)
    arrived = send_back(returned)
    summed = sum_weights(rows_in, grad_in, hidden, grad_pair, grad_scale)
    input_grad = lax.dot_general(
        dispatch_table,
        arrived.reshape(experts * capacity, model_width),
        (((0,), (0,)), ((), ())),
        preferred_element_type=jnp.float32,
    ).astype(jnp.bfloat16)
    return (input_grad, summed.reshape(1, share_rows, 3 * hidden_width))


def solution(mesh):
    split = Mesh(
        mesh.devices.reshape(4, 4, 2, mesh.shape["expert"]), ("dp_0", "dp_1", "dp_2", "expert")
    )
    placed = (
        P(DP_EXPERT, None),
        P(DP_EXPERT, None),
        P(DP_EXPERT, None),
        P(DP_EXPERT, None),
        P("expert", None, None),
    )
    return jax.shard_map(
        local,
        mesh=split,
        in_specs=placed,
        out_specs=(P(DP_EXPERT, None), P("expert", DP, None)),
        check_vma=False,
    )
```

profile of v0, /device:TPU:6, one launch (start us, length us, event | category | flops | bytes accessed | tf_op | source)
XLA Modules:
  0.0 406.6 jit_solution(18429964155232158776)
XLA Ops:
  7.2 0.0 copy-start
  7.2 0.0 reduce-scatter.5.cloned.1.call-start
  7.2 0.8 fusion.27
  8.0 0.2 reduce_window_sum.11
  8.2 0.8 select_reduce_fusion
  9.0 0.7 multiply_add_fusion
  9.7 0.0 copy-done
  9.7 0.4 fusion.12
  10.1 1.6 fusion.13
  11.7 0.2 pad_maximum_fusion
  11.9 223.6 %all_to_all.10 = bf16[32,16,2048]{2,1,0:T(8,128)(2,1)S(1)} all-to-all(bf16[32,16,2048]{2,1,0:T(8,128)(2,1)S(1)} %pad_maximum_fusion), channel_id=1, replica_groups=mesh['dp_0'=4,'dp_1'=4,'dp_2'=2,'expert'=32] {'expert'}, dimensions={0} | all-to-all | bytes 4194304 | tf_op jit(solution)/shard_map/all_to_all | solution.py:28
  235.5 1.5 slice_bitcast_fusion
  237.0 2.3 copy.12
  239.3 2.3 copy.13
  241.5 2.9 fusion.4
  244.5 0.0 copy-done.1
  244.5 2.5 fusion.22
  247.0 2.3 multiply_convert_fusion.4
  249.3 0.0 copy-done.2
  249.3 3.6 fusion.18
  252.9 4.9 %fusion.1 = bf16[2,16,64,1152]{3,2,0,1:T(8,128)(2,1)S(1)} fusion(f32[16,2,64,384]{3,2,1,0:T(8,128)} %fusion.22, f32[16,2,64,768]{3,2,1,0:T(8,128)} %fusion.18), kind=kLoop, calls=%fused_computation.2 | loop fusion | flops 7077888 | bytes 14155776 | tf_op jit(solution)/shard_map/transpose | solution.py:20
  257.8 2.5 copy.14
  260.3 0.0 reduce-scatter.5.cloned.1.call-update
  260.3 3.9 fusion.9
  264.2 7.3 %all-to-all-start.1 = ((bf16[32,8,2048]{2,1,0:T(8,128)(2,1)}), bf16[32,8,2048]{2,1,0:T(8,128)(2,1)S(1)}, u32[]{:S(2)}, u32[]{:S(2)}) async-start(bf16[32,8,2048]{2,1,0:T(8,128)(2,1)} %fusion.9), calls=%async_computation.1 | async-start | bytes 2097152 | tf_op jit(solution)/shard_map/all_to_all | solution.py:80
  271.5 0.0 reduce-scatter.7.cloned.1.call-start
  271.6 8.3 %reduce-scatter.5.cloned.1.call-done = bf16[16,64,1152]{2,1,0:T(8,128)(2,1)} async-done(((bf16[32,64,1152]{2,1,0:T(8,128)(2,1)}), bf16[16,64,1152]{2,1,0:T(8,128)(2,1)}) %reduce-scatter.5.cloned.1.call-update) | async-done | bytes 2359312 | tf_op jit(solution)/shard_map/reduce_scatter | solution.py:21
  279.8 0.0 reduce-scatter.7.cloned.1.call-update
  279.8 96.9 %all-to-all-done.1 = bf16[32,8,2048]{2,1,0:T(8,128)(2,1)S(1)} async-done(((bf16[32,8,2048]{2,1,0:T(8,128)(2,1)}), bf16[32,8,2048]{2,1,0:T(8,128)(2,1)S(1)}, u32[]{:S(2)}, u32[]{:S(2)}) %all-to-all-start.1) | async-done | bytes 1048608 | tf_op jit(solution)/shard_map/all_to_all | solution.py:80
  376.8 1.1 convolution_convert_fusion.2
  377.9 20.2 %reduce-scatter.7.cloned.1.call-done = bf16[1,64,1152]{2,1,0:T(8,128)(2,1)} async-done(((bf16[16,64,1152]{2,1,0:T(8,128)(2,1)}), bf16[1,64,1152]{2,1,0:T(8,128)(2,1)}) %reduce-scatter.7.cloned.1.call-update) | async-done | bytes 147472
  398.1 1.6 convert_element_type.50
  (2 shorter events, 0.0 us)
Async XLA Ops:
  7.2 2.5 copy-start
  7.2 272.6 %reduce-scatter.5.cloned.1.call-start = ((), (), s32[]{:S(2)}) async-start(), calls=%async_computation.4 | async-start | bytes 7077888 | tf_op jit(solution)/shard_map/reduce_scatter | solution.py:21
  241.5 3.0 copy-start.1
  247.0 2.3 copy-start.2
  264.2 112.6 %all-to-all-start.1 = ((bf16[32,8,2048]{2,1,0:T(8,128)(2,1)}), bf16[32,8,2048]{2,1,0:T(8,128)(2,1)S(1)}, u32[]{:S(2)}, u32[]{:S(2)}) async-start(bf16[32,8,2048]{2,1,0:T(8,128)(2,1)} %fusion.9), calls=%async_computation.1 | async-start | bytes 2097152 | tf_op jit(solution)/shard_map/all_to_all | solution.py:80
  271.5 126.6 %reduce-scatter.7.cloned.1.call-start = ((), (), s32[]{:S(2)}) async-start(), calls=%async_computation.5 | async-start | bytes 2506752
Sparse Core Ops, SparseCore 0:
  260.4 19.3 reduce-scatter.4
  285.2 112.9 reduce-scatter.6
where the time goes:
time: 407 us
  blocking collectives  224 us (55%)
  waiting for transfers between devices  125 us (31%)
  matrix products  18.3 us (4%)
  between operations  14.1 us (3%)
  other arithmetic  9.23 us (2%)
  local copies, waits for them, and re-layouts  8.52 us (2%)
  starting transfers between devices  7.39 us (2%)
    all_to_all x1, blocking collectives, side_by_side(): lax.all_to_all(both, axis, split_axis=split_dim, concat_axis=concat_dim,...  224 us
    all_to_all x1, waiting for transfers between devices, send_back(): lax.all_to_all(returned, 'expert', split_axis=0, concat_axis=0, tiled=True)  96.9 us
    unnamed x3, waiting for transfers between devices  20.2 us
    reduce_scatter x1, waiting for transfers between devices, scatter_pairs(): parts = lax.psum_scatter(parts, core, scatter_dimension=0, tiled=True)  8.26 us
  transfers between devices with their start and end apart: 3, of which 3 were waited for; matrix products, arithmetic and copies ran while one was open for 1% of the time, Pallas kernels for 0%

commit v1 on v0

--- a/solution.py
+++ b/solution.py
@@ -6,20 +6,6 @@
 
 DP = ("dp_0", "dp_1", "dp_2")
 DP_EXPERT = ("dp_0", "dp_1", "dp_2", "expert")
-
-
-def in_blocks(value, dim, length):
-    before, after = (value.shape[:dim], value.shape[dim + 1 :])
-    return jnp.moveaxis(value.reshape(*before, length, -1, *after), dim, 0)
-
-
-def scatter_pairs(value, chips, core, dim):
-    sizes = (lax.axis_size(chips), lax.axis_size(core))
-    parts = in_blocks(value, dim, sizes[0] * sizes[1])
-    inside = parts.shape[1:]
-    parts = parts.reshape(*sizes, *inside).swapaxes(0, 1).reshape(-1, *inside)
-    parts = lax.psum_scatter(parts, core, scatter_dimension=0, tiled=True)
-    return lax.psum_scatter(parts, chips, scatter_dimension=0, tiled=True)[0]
 
 
 def side_by_side(arrays, axis, split_dim, concat_dim, along):
@@ -68,16 +54,10 @@
 
 
 def sum_weights(rows_in, grad_in, hidden, grad_pair, grad_scale):
-    return scatter_pairs(
-        weight_term(rows_in, grad_in, hidden, grad_pair, grad_scale).astype(jnp.bfloat16),
-        ("dp_0", "dp_1"),
-        "dp_2",
-        0,
-    ).astype(jnp.float32)
-
-
-def send_back(returned):
-    return lax.all_to_all(returned, "expert", split_axis=0, concat_axis=0, tiled=True)
+    term = weight_term(rows_in, grad_in, hidden, grad_pair, grad_scale).astype(jnp.bfloat16)
+    bands = term.reshape(lax.axis_size(DP), -1, term.shape[1])
+    bands = lax.all_to_all(bands, DP, split_axis=0, concat_axis=0, tiled=True)
+    return lax.psum_scatter(bands, "expert", scatter_dimension=0, tiled=False).astype(jnp.float32)
 
 
 def local(tokens, out_grad, gate_prob, routing, expert_weights):
@@ -87,8 +67,11 @@
     capacity = 2 * tok_dev // experts
     share_rows = model_width // replicas
     grad_scale = float(tok_dev * replicas) ** (-0.5)
-    weights = expert_weights[0]
-    hidden_width = weights.shape[1] // 3
+    width = expert_weights.shape[2]
+    band = lax.dynamic_slice_in_dim(
+        expert_weights[0], lax.axis_index(DP) * share_rows, share_rows, 0
+    )
+    bands = lax.all_gather(band, "expert", axis=0, tiled=False)
     scaled = (gate_prob * out_grad.astype(jnp.float32)).astype(jnp.bfloat16)
     slot_index = slot_of(routing[:, 0], capacity, experts)
     dispatch_table = (
@@ -104,20 +87,22 @@
         .astype(jnp.bfloat16)
         .reshape(experts, capacity, model_width)
     )
-    recv_x, recv_g = side_by_side((send_x, send_g), "expert", 0, 0, 1)
+    recv_x, recv_g = side_by_side((send_x, send_g), DP, 0, 0, 1)
     rows_in = recv_x.reshape(experts * capacity, model_width)
     grad_in = recv_g.reshape(experts * capacity, model_width)
+    weights = lax.all_to_all(bands, DP, split_axis=0, concat_axis=0, tiled=True)
+    weights = weights.reshape(model_width, width)
     returned, hidden, grad_pair = expert_rows(weights, rows_in, grad_in)
     returned = returned.reshape(experts, capacity, model_width)
-    arrived = send_back(returned)
     summed = sum_weights(rows_in, grad_in, hidden, grad_pair, grad_scale)
+    arrived = lax.all_to_all(returned, DP, split_axis=0, concat_axis=0, tiled=True)
     input_grad = lax.dot_general(
         dispatch_table,
         arrived.reshape(experts * capacity, model_width),
         (((0,), (0,)), ((), ())),
         preferred_element_type=jnp.float32,
     ).astype(jnp.bfloat16)
-    return (input_grad, summed.reshape(1, share_rows, 3 * hidden_width))
+    return (input_grad, summed.reshape(1, share_rows, width))
 
 
 def solution(mesh):

time: 407 us -> 449 us (1.10)
  the two profiles are of different devices: /device:TPU:6 before, /device:TPU:4 now
where the time goes in v1:
time: 449 us; the launch traced here: 448 us
  waiting for transfers between devices  266 us (59%)
  blocking collectives  127 us (28%)
  matrix products  17.4 us (4%)
  between operations  14.1 us (3%)
  other arithmetic  9.17 us (2%)
  local copies, waits for them, and re-layouts  7.73 us (2%)
  starting transfers between devices  7.35 us (2%)
    reduce_scatter x1, waiting for transfers between devices, sum_weights(): lax.psum_scatter(bands, 'expert', scatter_dimension=0, tiled=False)  110 us
    all_gather x1, waiting for transfers between devices, local(): bands = lax.all_gather(band, 'expert', axis=0, tiled=False)  107 us
    all_to_all x1, blocking collectives, sum_weights(): bands = lax.all_to_all(bands, DP, split_axis=0, concat_axis=0, tiled=True)  63.2 us
    all_to_all x1, waiting for transfers between devices, local(): weights = lax.all_to_all(bands, DP, split_axis=0, concat_axis=0, tiled=True)  48.9 us
    all_to_all x1, blocking collectives, side_by_side(): lax.all_to_all(both, axis, split_axis=split_dim, concat_axis=concat_dim,...  42.4 us
    all_to_all x1, blocking collectives, local(): lax.all_to_all(returned, DP, split_axis=0, concat_axis=0, tiled=True)  21.3 us
  transfers between devices with their start and end apart: 3, of which 3 were waited for; matrix products, arithmetic and copies ran while one was open for 3% of the time, Pallas kernels for 0%

profile of v1, /device:TPU:4, one launch (start us, length us, event | category | flops | bytes accessed | tf_op | source)
XLA Modules:
  0.0 448.5 jit_solution(10413585334546653297)
XLA Ops:
  7.2 0.0 copy-start
  7.2 0.0 all-gather.2.cloned.1.call-start
  7.2 1.6 constant_dynamic-slice_fusion
  8.9 0.0 all-gather.2.cloned.1.call-update
  8.9 0.7 fusion.26
  9.6 0.2 reduce_window_sum.11
  9.8 0.8 select_reduce_fusion
  10.6 0.7 multiply_add_fusion
  11.3 0.0 copy-done
  11.3 0.4 fusion.11
  11.7 1.6 fusion.12
  13.3 0.2 pad_maximum_fusion
  13.6 42.4 %all_to_all.20 = bf16[32,16,2048]{2,1,0:T(8,128)(2,1)S(1)} all-to-all(bf16[32,16,2048]{2,1,0:T(8,128)(2,1)S(1)} %pad_maximum_fusion), channel_id=1, replica_groups=mesh['dp_0'=4,'dp_1'=4,'dp_2'=2,'expert'=32] {'dp_0','dp_1','dp_2'}, dimensions={0} | all-to-all | bytes 4194304 | tf_op jit(solution)/shard_map/all_to_all | solution.py:14
  56.0 106.8 %all-gather.2.cloned.1.call-done = bf16[32,64,1152]{2,1,0:T(8,128)(2,1)} async-done(((bf16[1,64,1152]{2,1,0:T(8,128)(2,1)}), bf16[32,64,1152]{2,1,0:T(8,128)(2,1)}) %all-gather.2.cloned.1.call-update) | async-done | bytes 4718608 | tf_op jit(solution)/shard_map/all_gather | solution.py:74
  162.7 7.3 %all-to-all-start.1 = ((bf16[32,64,1152]{2,1,0:T(8,128)(2,1)}), bf16[32,64,1152]{2,1,0:T(8,128)(2,1)}, u32[]{:S(2)}, u32[]{:S(2)}) async-start(bf16[32,64,1152]{2,1,0:T(8,128)(2,1)} %all-gather.2.cloned.1.call-done), calls=%async_computation.1 | async-start | bytes 9437184 | tf_op jit(solution)/shard_map/all_to_all | solution.py:93
  170.0 0.0 reduce-scatter.2.cloned.1.call-start
  170.0 1.5 slice_bitcast_fusion
  171.6 2.3 copy.9
  173.8 2.3 copy.10
  176.1 48.9 %all-to-all-done.1 = bf16[32,64,1152]{2,1,0:T(8,128)(2,1)} async-done(((bf16[32,64,1152]{2,1,0:T(8,128)(2,1)}), bf16[32,64,1152]{2,1,0:T(8,128)(2,1)}, u32[]{:S(2)}, u32[]{:S(2)}) %all-to-all-start.1) | async-done | bytes 4718624 | tf_op jit(solution)/shard_map/all_to_all | solution.py:93
  225.0 2.9 fusion.3
  228.0 2.6 fusion.21
  230.6 2.3 multiply_convert_fusion.4
  232.9 3.6 fusion.17
  236.5 4.9 %fusion = bf16[32,64,1152]{2,1,0:T(8,128)(2,1)S(1)} fusion(f32[32,64,384]{2,1,0:T(8,128)} %fusion.21, f32[32,64,768]{2,1,0:T(8,128)} %fusion.17), kind=kLoop, calls=%fused_computation.1 | loop fusion | flops 7077888 | bytes 14155776 | tf_op jit(solution)/shard_map/convert_element_type | solution.py:57
  241.4 63.2 %all_to_all.21 = bf16[32,64,1152]{2,1,0:T(8,128)(2,1)} all-to-all(bf16[32,64,1152]{2,1,0:T(8,128)(2,1)S(1)} %fusion), channel_id=1, replica_groups=mesh['dp_0'=4,'dp_1'=4,'dp_2'=2,'expert'=32] {'dp_0','dp_1','dp_2'}, dimensions={0} | all-to-all | bytes 9437184 | tf_op jit(solution)/shard_map/all_to_all | solution.py:59
  304.6 0.0 reduce-scatter.2.cloned.1.call-update
  304.6 2.9 fusion.8
  307.5 21.3 %all_to_all.22 = bf16[32,8,2048]{2,1,0:T(8,128)(2,1)S(1)} all-to-all(bf16[32,8,2048]{2,1,0:T(8,128)(2,1)S(1)} %fusion.8), channel_id=1, replica_groups=mesh['dp_0'=4,'dp_1'=4,'dp_2'=2,'expert'=32] {'dp_0','dp_1','dp_2'}, dimensions={0} | all-to-all | bytes 2097152 | tf_op jit(solution)/shard_map/all_to_all | solution.py:98
  328.8 1.1 convolution_convert_fusion.2
  329.9 110.1 %reduce-scatter.2.cloned.1.call-done = bf16[1,64,1152]{2,1,0:T(8,128)(2,1)} async-done(((bf16[32,64,1152]{2,1,0:T(8,128)(2,1)}), bf16[1,64,1152]{2,1,0:T(8,128)(2,1)}) %reduce-scatter.2.cloned.1.call-update) | async-done | bytes 147472 | tf_op jit(solution)/shard_map/reduce_scatter | solution.py:60
  440.0 1.6 convert_element_type.50
  (4 shorter events, 0.0 us)
Async XLA Ops:
  7.2 4.1 copy-start
  7.2 155.5 %all-gather.2.cloned.1.call-start = ((), (), s32[]{:S(2)}) async-start(), calls=%async_computation.5 | async-start | bytes 4866048 | tf_op jit(solution)/shard_map/all_gather | solution.py:74
  162.7 62.3 %all-to-all-start.1 = ((bf16[32,64,1152]{2,1,0:T(8,128)(2,1)}), bf16[32,64,1152]{2,1,0:T(8,128)(2,1)}, u32[]{:S(2)}, u32[]{:S(2)}) async-start(bf16[32,64,1152]{2,1,0:T(8,128)(2,1)} %all-gather.2.cloned.1.call-done), calls=%async_computation.1 | async-start | bytes 9437184 | tf_op jit(solution)/shard_map/all_to_all | solution.py:93
  170.0 270.0 %reduce-scatter.2.cloned.1.call-start = ((), (), s32[]{:S(2)}) async-start(), calls=%async_computation.6 | async-start | bytes 4866048 | tf_op jit(solution)/shard_map/reduce_scatter | solution.py:60
  225.0 3.0 copy-start.1
  230.6 2.3 copy-start.2
Sparse Core Ops, SparseCore 0:
  11.2 151.4 all-gather.1
  304.7 135.2 reduce-scatter.1

commit v2 on v1

v2 whole, which is shorter than its diff:
```python
import functools

import jax
import jax.numpy as jnp
from jax import lax
from jax.experimental import pallas as pl
from jax.experimental.pallas import tpu as pltpu
from jax.sharding import PartitionSpec as P

MESH = pl.DeviceIdType.MESH
CHUNKS = 64


def place(n, planes):
    mine = lax.axis_index("dp")
    plane = lax.axis_index("expert")
    expert = mine // 2 + (n // 2) * (mine % 2)
    return plane, mine, (plane - expert + planes) % planes


def meet(n, planes, plane, mine):
    barrier = pltpu.get_barrier_semaphore()

    @pl.loop(1, n)
    def _(k):
        pl.semaphore_signal(
            barrier, inc=1, device_id=((mine + k) % n, plane), device_id_type=MESH
        )

    for step in (1, planes - 1):
        pl.semaphore_signal(
            barrier, inc=1, device_id=(mine, (plane + step) % planes), device_id_type=MESH
        )
    pl.semaphore_wait(barrier, n + 1)


def exchange(n, plane, mine, source, target, send_sem, recv_sem):
    def copy(k):
        peer = (mine + k) % n
        return pltpu.make_async_remote_copy(
            src_ref=source.at[peer],
            dst_ref=target.at[mine],
            send_sem=send_sem.at[k],
            recv_sem=recv_sem.at[k],
            device_id=(peer, plane),
            device_id_type=MESH,
        )

    return copy, pltpu.make_async_copy(source.at[mine], target.at[mine], recv_sem.at[0])


def gather_kernel(n, planes, own_ref, rows_ref, weights_ref, recv_ref, w_send, w_down, w_recv, t_send, t_recv):
    plane, mine, far = place(n, planes)
    half = planes // 2
    origin = far == 0
    onward = jnp.logical_and(far != half, far != half + 1)
    step = jnp.where(far <= half, 1, planes - 1)
    depth = weights_ref.shape[0] // CHUNKS

    def chunk(k):
        return pl.ds(pl.multiple_of(k * depth, depth), depth)

    def local(k):
        return pltpu.make_async_copy(own_ref.at[chunk(k)], weights_ref.at[chunk(k)], w_recv.at[k])

    def hop(k, by, sem):
        return pltpu.make_async_remote_copy(
            src_ref=weights_ref.at[chunk(k)],
            dst_ref=weights_ref.at[chunk(k)],
            send_sem=sem.at[k],
            recv_sem=w_recv.at[k],
            device_id=(mine, (plane + by) % planes),
            device_id_type=MESH,
        )

    @pl.when(origin)
    def _():
        @pl.loop(0, CHUNKS)
        def _(k):
            local(k).start()

    meet(n, planes, plane, mine)
    copy, stay = exchange(n, plane, mine, rows_ref, recv_ref, t_send, t_recv)
    stay.start()

    @pl.loop(1, n)
    def _(k):
        copy(k).start()

    @pl.loop(0, CHUNKS)
    def _(k):
        local(k).wait()

        @pl.when(onward)
        def _():
            hop(k, step, w_send).start()

        @pl.when(origin)
        def _():
            hop(k, planes - 1, w_down).start()

    stay.wait()

    @pl.loop(1, n)
    def _(k):
        copy(k).wait()

    @pl.when(onward)
    def _():
        @pl.loop(0, CHUNKS)
        def _(k):
            hop(k, step, w_send).wait_send()

    @pl.when(origin)
    def _():
        @pl.loop(0, CHUNKS)
        def _(k):
            hop(k, planes - 1, w_down).wait_send()


def reduce_kernel(
    n, planes, part_ref, back_ref, band_ref, recv_ref, inbox, total, c_send, c_recv, b_send, b_recv, t_send, t_recv
):
    plane, mine, far = place(n, planes)
    half = planes // 2
    origin = far == 0
    first = jnp.logical_or(far == half, far == half + 1)
    middle = jnp.logical_not(jnp.logical_or(origin, first))
    step = jnp.where(far <= half, planes - 1, 1)
    side = jnp.where(far == planes - 1, 1, 0)
    depth = part_ref.shape[0] // CHUNKS
    pieces = band_ref.shape[0] // depth

    def chunk(k):
        return pl.ds(pl.multiple_of(k * depth, depth), depth)

    def hop(k, to, source):
        return pltpu.make_async_remote_copy(
            src_ref=source.at[chunk(k)],
            dst_ref=inbox.at[to, chunk(k)],
            send_sem=c_send.at[k],
            recv_sem=c_recv.at[to, k],
            device_id=(mine, (plane + step) % planes),
            device_id_type=MESH,
        )

    def spread(k):
        return pltpu.make_async_remote_copy(
            src_ref=total.at[chunk(k)],
            dst_ref=band_ref.at[chunk(k % pieces)],
            send_sem=b_send.at[k],
            recv_sem=b_recv.at[k % pieces],
            device_id=(k // pieces, plane),
            device_id_type=MESH,
        )

    def keep(k):
        return pltpu.make_async_copy(
            total.at[chunk(k)], band_ref.at[chunk(k % pieces)], b_recv.at[k % pieces]
        )

    meet(n, planes, plane, mine)

    @pl.when(first)
    def _():
        @pl.loop(0, CHUNKS)
        def _(k):
            hop(k, side, part_ref).start()

    copy, stay = exchange(n, plane, mine, back_ref, recv_ref, t_send, t_recv)
    stay.start()

    @pl.loop(1, n)
    def _(k):
        copy(k).start()

    @pl.when(middle)
    def _():
        @pl.loop(0, CHUNKS)
        def _(k):
            hop(k, 0, total).wait_recv()
            rows = chunk(k)
            total[rows, :] = (
                inbox[0, rows, :].astype(jnp.float32) + part_ref[rows, :].astype(jnp.float32)
            ).astype(jnp.bfloat16)
            hop(k, side, total).start()

    @pl.when(origin)
    def _():
        @pl.loop(0, CHUNKS)
        def _(k):
            hop(k, 0, total).wait_recv()
            hop(k, 1, total).wait_recv()
            rows = chunk(k)
            total[rows, :] = (
                inbox[0, rows, :].astype(jnp.float32)
                + inbox[1, rows, :].astype(jnp.float32)
                + part_ref[rows, :].astype(jnp.float32)
            ).astype(jnp.bfloat16)

            @pl.when(k // pieces != mine)
            def _():
                spread(k).start()

            @pl.when(k // pieces == mine)
            def _():
                keep(k).start()

    stay.wait()

    @pl.loop(1, n)
    def _(k):
        copy(k).wait()

    @pl.when(jnp.logical_not(origin))
    def _():
        @pl.loop(0, CHUNKS)
        def _(k):
            hop(k, side, total).wait_send()

    @pl.when(origin)
    def _():
        @pl.loop(0, CHUNKS)
        def _(k):
            @pl.when(k // pieces != mine)
            def _():
                spread(k).wait_send()

    @pl.loop(0, pieces)
    def _(k):
        keep(k).wait()


def slot_of(route_block, capacity, experts):
    onehot = (route_block[:, None] == jnp.arange(experts, dtype=jnp.int32)[None, :]).astype(
        jnp.int32
    )
    before = jnp.cumsum(onehot, axis=0) - onehot
    position = jnp.sum(before * onehot, axis=1)
    holder = 2 * (route_block % (experts // 2)) + route_block // (experts // 2)
    return holder * capacity + position


def expert_rows(weights, rows_in, grad_in):
    hidden_width = weights.shape[1] // 3
    pair_weights = weights[:, : 2 * hidden_width]
    down_weights = weights[:, 2 * hidden_width :]
    pre_act = jnp.dot(rows_in, pair_weights, preferred_element_type=jnp.float32)
    pre_gate = pre_act[:, :hidden_width]
    pre_up = pre_act[:, hidden_width:]
    sigmoid_gate = jax.nn.sigmoid(pre_gate)
    active = pre_gate * sigmoid_gate
    hidden = (active * pre_up).astype(jnp.bfloat16)
    grad_hidden = jnp.dot(grad_in, down_weights, preferred_element_type=jnp.float32)
    grad_gate = grad_hidden * pre_up * (sigmoid_gate * (1.0 + pre_gate * (1.0 - sigmoid_gate)))
    grad_up = grad_hidden * active
    grad_pair = jnp.concatenate(
        [grad_gate.astype(jnp.bfloat16), grad_up.astype(jnp.bfloat16)], axis=1
    )
    returned = lax.dot_general(
        grad_pair, pair_weights, (((1,), (1,)), ((), ())), preferred_element_type=jnp.float32
    )
    return (returned.astype(jnp.bfloat16), hidden, grad_pair)


def weight_term(rows_in, grad_in, hidden, grad_pair, grad_scale):
    contract = (((0,), (0,)), ((), ()))
    first_part = lax.dot_general(rows_in, grad_pair, contract, preferred_element_type=jnp.float32)
    second = lax.dot_general(grad_in, hidden, contract, preferred_element_type=jnp.float32)
    return grad_scale * jnp.concatenate([first_part, second], axis=1)


def local(tokens, out_grad, gate_prob, routing, expert_weights):
    tok_dev, model_width = tokens.shape
    planes = lax.axis_size("expert")
    n = lax.axis_size("dp")
    capacity = 2 * tok_dev // planes
    share_rows = model_width // n
    grad_scale = float(tok_dev * n) ** (-0.5)
    width = expert_weights.shape[2]
    vmem = pl.BlockSpec(memory_space=pltpu.VMEM)
    dma = pltpu.SemaphoreType.DMA
    scaled = (gate_prob * out_grad.astype(jnp.float32)).astype(jnp.bfloat16)
    slot_index = slot_of(routing[:, 0], capacity, planes)
    dispatch_table = (
        jnp.arange(planes * capacity, dtype=jnp.int32)[:, None] == slot_index[None, :]
    ).astype(jnp.bfloat16)

    def spread_out(rows):
        return (
            jnp.dot(dispatch_table, rows, preferred_element_type=jnp.float32)
            .astype(jnp.bfloat16)
            .reshape(n, capacity, model_width)
        )

    send = jnp.concatenate([spread_out(tokens), spread_out(scaled)], axis=1)
    weights, received = pl.pallas_call(
        functools.partial(gather_kernel, n, planes),
        out_shape=(
            jax.ShapeDtypeStruct((model_width, width), jnp.bfloat16),
            jax.ShapeDtypeStruct(send.shape, jnp.bfloat16),
        ),
        in_specs=[pl.BlockSpec(memory_space=pl.ANY), vmem],
        out_specs=(vmem, vmem),
        scratch_shapes=[dma((CHUNKS,)), dma((CHUNKS,)), dma((CHUNKS,)), dma((n,)), dma((n,))],
        compiler_params=pltpu.CompilerParams(collective_id=0, has_side_effects=True),
    )(expert_weights[0], send)
    rows_in = received[:, :capacity].reshape(n * capacity, model_width)
    grad_in = received[:, capacity:].reshape(n * capacity, model_width)
    returned, hidden, grad_pair = expert_rows(weights, rows_in, grad_in)
    returned = returned.reshape(n, capacity, model_width)
    term = weight_term(rows_in, grad_in, hidden, grad_pair, grad_scale).astype(jnp.bfloat16)
    band, arrived = pl.pallas_call(
        functools.partial(reduce_kernel, n, planes),
        out_shape=(
            jax.ShapeDtypeStruct((share_rows, width), jnp.bfloat16),
            jax.ShapeDtypeStruct(returned.shape, jnp.bfloat16),
        ),
        in_specs=[vmem, vmem],
        out_specs=(vmem, vmem),
        scratch_shapes=[
            pltpu.VMEM((2, model_width, width), jnp.bfloat16),
            pltpu.VMEM((model_width, width), jnp.bfloat16),
            dma((CHUNKS,)),
            dma((2, CHUNKS)),
            dma((CHUNKS,)),
            dma((CHUNKS // n,)),
            dma((n,)),
            dma((n,)),
        ],
        compiler_params=pltpu.CompilerParams(collective_id=1, has_side_effects=True),
    )(term, returned)
    input_grad = lax.dot_general(
        dispatch_table,
        arrived.reshape(n * capacity, model_width),
        (((0,), (0,)), ((), ())),
        preferred_element_type=jnp.float32,
    ).astype(jnp.bfloat16)
    return (input_grad, band.astype(jnp.float32).reshape(1, share_rows, width))


def solution(mesh):
    both = P(("dp", "expert"), None)
    return jax.shard_map(
        local,
        mesh=mesh,
        in_specs=(both, both, both, both, P("expert", None, None)),
        out_specs=(both, P("expert", "dp", None)),
        check_vma=False,
    )
```

time: 449 us -> 275 us (0.61)
  the two profiles are of different devices: /device:TPU:4 before, /device:TPU:31 now
where the time goes in v2:
time: 275 us
  Pallas kernels  247 us (90%)
  matrix products  14.9 us (5%)
  other arithmetic  11.4 us (4%)
    pallas_call x1, Pallas kernels, local(): pl.pallas_call(functools.partial(reduce_kernel, n, planes), out_shape=(ja...  167 us
    pallas_call x1, Pallas kernels, local(): pl.pallas_call(functools.partial(gather_kernel, n, planes), out_shape=(ja...  80 us
    convert_element_type x1, other arithmetic, local(): weight_term(rows_in, grad_in, hidden, grad_pair, grad_scale)  5.79 us

profile of v2, /device:TPU:31, one launch (start us, length us, event | category | flops | bytes accessed | tf_op | source)
XLA Modules:
  0.0 274.8 jit_solution(1689499727406840466)
XLA Ops:
  0.6 0.0 copy-start
  0.6 0.8 fusion.31
  1.4 0.2 reduce_window_sum.11
  1.6 0.8 select_reduce_fusion
  2.4 0.7 multiply_add_fusion
  3.1 1.6 fusion.12
  4.7 0.0 copy-done
  4.7 0.4 fusion.11
  5.1 1.5 pad_maximum_fusion.rows_ref
  6.6 80.0 %shard_map.68 = (bf16[2048,1152]{1,0:T(8,128)(2,1)}, bf16[32,16,2048]{2,1,0:T(8,128)(2,1)}) custom-call(bf16[2048,1152]{1,0:T(8,128)(2,1)} %bitcast.29, bf16[32,16,2048]{2,1,0:T(8,128)(2,1)} %pad_maximum_fusion.rows_ref), custom_call_target="tpu_custom_call" | custom-call | tf_op jit(solution)/shard_map/pallas_call | solution.py:297
  86.7 0.0 copy-start.1
  86.7 0.0 copy-start.2
  86.7 3.3 %fusion.3 = f32[256,768]{1,0:T(8,128)S(1)} fusion(bf16[2048,1152]{1,0:T(8,128)(2,1)} %get-tuple-element.7, bf16[32,16,2048]{2,1,0:T(8,128)(2,1)} %get-tuple-element.6), kind=kOutput, calls=%fused_computation.4 | convolution fusion | flops 805306368 | bytes 4980736 | tf_op jit(solution)/shard_map/dot_general | solution.py:248
  90.0 0.0 copy-done.1
  90.0 0.9 copy-done.2
  90.9 0.8 multiply_convert_fusion.4
  91.7 2.0 fusion.8.back_ref
  93.7 0.8 fusion.16
  94.5 3.7 %fusion.19 = f32[2048,768]{1,0:T(8,128)} fusion(bf16[32,16,2048]{2,1,0:T(8,128)(2,1)S(1)} %copy-done.1, bf16[256,384]{1,0:T(8,128)(2,1)S(1)} %get-tuple-element.11, bf16[256,384]{1,0:T(8,128)(2,1)S(1)} %get-tuple-element.10), kind=kOutput, calls=%fused_computation.20 | convolution fusion | flops 806092800 | bytes 7733248 | tf_op jit(solution)/shard_map/dot_general | solution.py:268
  98.2 5.8 %fusion.part_ref = bf16[2048,1152]{1,0:T(8,128)(2,1)} fusion(f32[2048,384]{1,0:T(8,128)S(1)} %fusion.16, f32[2048,768]{1,0:T(8,128)} %fusion.19), kind=kLoop, calls=%fused_computation.1 | loop fusion | flops 7077888 | bytes 14155776 | tf_op jit(solution)/shard_map/convert_element_type | solution.py:312
  104.0 166.8 %shard_map.69 = (bf16[64,1152]{1,0:T(8,128)(2,1)}, bf16[32,8,2048]{2,1,0:T(8,128)(2,1)}) custom-call(bf16[2048,1152]{1,0:T(8,128)(2,1)} %fusion.part_ref, bf16[32,8,2048]{2,1,0:T(8,128)(2,1)} %fusion.8.back_ref), custom_call_target="tpu_custom_call" | custom-call | tf_op jit(solution)/shard_map/pallas_call | solution.py:313
  270.8 2.4 convolution_convert_fusion.2
  273.2 1.6 bitcast_convert_fusion
Async XLA Ops:
  0.6 4.1 %copy-start = (bf16[128,2048]{1,0:T(8,128)(2,1)S(1)}, bf16[128,2048]{1,0:T(8,128)(2,1)}, u32[]{:S(2)}) copy-start(bf16[128,2048]{1,0:T(8,128)(2,1)} %param.5) | copy-start | bytes 1572868
  86.7 3.4 %copy-start.1 = (bf16[32,16,2048]{2,1,0:T(8,128)(2,1)S(1)}, bf16[32,16,2048]{2,1,0:T(8,128)(2,1)}, u32[]{:S(2)}) copy-start(bf16[32,16,2048]{2,1,0:T(8,128)(2,1)} %get-tuple-element.6) | copy-start | bytes 6291460
  86.7 4.2 %copy-start.2 = (bf16[2048,1152]{1,0:T(8,128)(2,1)S(1)}, bf16[2048,1152]{1,0:T(8,128)(2,1)}, u32[]{:S(2)}) copy-start(bf16[2048,1152]{1,0:T(8,128)(2,1)} %get-tuple-element.7) | copy-start | bytes 14155780

commit v3 on v2

v3 whole, which is shorter than its diff:
```python
import functools

import jax
import jax.numpy as jnp
from jax import lax
from jax.experimental import pallas as pl
from jax.experimental.pallas import tpu as pltpu
from jax.sharding import PartitionSpec as P

MESH = pl.DeviceIdType.MESH
CHUNKS = 128
TILES = 4
KERNEL_MIB = 48


def place(n, planes):
    mine = lax.axis_index("dp")
    plane = lax.axis_index("expert")
    expert = mine // 2 + (n // 2) * (mine % 2)
    return plane, mine, (plane - expert + planes) % planes


def meet(n, planes, plane, mine):
    barrier = pltpu.get_barrier_semaphore()

    @pl.loop(1, n)
    def _(k):
        pl.semaphore_signal(
            barrier, inc=1, device_id=((mine + k) % n, plane), device_id_type=MESH
        )

    for step in (1, planes - 1):
        pl.semaphore_signal(
            barrier, inc=1, device_id=(mine, (plane + step) % planes), device_id_type=MESH
        )
    pl.semaphore_wait(barrier, n + 1)


def exchange(n, plane, mine, source, target, send_sem, recv_sem):
    rows = source.shape[0] // n

    def block(k):
        return pl.ds(pl.multiple_of(k * rows, rows), rows)

    def copy(k):
        peer = (mine + k) % n
        return pltpu.make_async_remote_copy(
            src_ref=source.at[block(peer)],
            dst_ref=target.at[block(mine)],
            send_sem=send_sem.at[k],
            recv_sem=recv_sem.at[k],
            device_id=(peer, plane),
            device_id_type=MESH,
        )

    stay = pltpu.make_async_copy(source.at[block(mine)], target.at[block(mine)], recv_sem.at[0])
    return copy, stay


def hidden_grads(weights_ref, x_ref, g_ref):
    depth, width = weights_ref.shape
    unit, tile = width // 3, depth // TILES
    pair = 2 * unit
    pre = grad_hidden = None
    for t in range(TILES):
        rows = slice(t * tile, (t + 1) * tile)
        one = jnp.dot(x_ref[:, rows], weights_ref[rows, :pair], preferred_element_type=jnp.float32)
        two = jnp.dot(g_ref[:, rows], weights_ref[rows, pair:], preferred_element_type=jnp.float32)
        pre = one if pre is None else pre + one
        grad_hidden = two if grad_hidden is None else grad_hidden + two
    pre_gate, pre_up = pre[:, :unit], pre[:, unit:]
    sigmoid_gate = jax.nn.sigmoid(pre_gate)
    active = pre_gate * sigmoid_gate
    hidden = (active * pre_up).astype(jnp.bfloat16)
    grad_gate = grad_hidden * pre_up * (sigmoid_gate * (1.0 + pre_gate * (1.0 - sigmoid_gate)))
    grad_up = grad_hidden * active
    grad_pair = jnp.concatenate(
        [grad_gate.astype(jnp.bfloat16), grad_up.astype(jnp.bfloat16)], axis=1
    )
    return hidden, grad_pair


def expert_kernel(
    n, planes, grad_scale, own_ref, x_ref, g_ref, band_ref, arrived_ref,
    weights, x_in, g_in, part, back, inbox, total,
    w_send, w_down, w_recv, c_send, c_recv, b_send, b_recv, t_send, t_recv,
):
    plane, mine, far = place(n, planes)
    half = planes // 2
    origin = far == 0
    end = jnp.logical_or(far == half, far == half + 1)
    up = jnp.where(far <= half, 1, planes - 1)
    home = jnp.where(far <= half, planes - 1, 1)
    side = jnp.where(far == planes - 1, 1, 0)
    depth = weights.shape[0] // CHUNKS
    tile = weights.shape[0] // TILES
    pair = 2 * weights.shape[1] // 3
    pieces = band_ref.shape[0] // depth

    def chunk(k):
        return pl.ds(pl.multiple_of(k * depth, depth), depth)

    def local(k):
        return pltpu.make_async_copy(own_ref.at[chunk(k)], weights.at[chunk(k)], w_recv.at[k])

    def out(k, by, sem):
        return pltpu.make_async_remote_copy(
            src_ref=weights.at[chunk(k)],
            dst_ref=weights.at[chunk(k)],
            send_sem=sem.at[k],
            recv_sem=w_recv.at[k],
            device_id=(mine, (plane + by) % planes),
            device_id_type=MESH,
        )

    def hop(k, to, source):
        return pltpu.make_async_remote_copy(
            src_ref=source.at[chunk(k)],
            dst_ref=inbox.at[to, chunk(k)],
            send_sem=c_send.at[k],
            recv_sem=c_recv.at[to, k],
            device_id=(mine, (plane + home) % planes),
            device_id_type=MESH,
        )

    def spread(k):
        return pltpu.make_async_remote_copy(
            src_ref=total.at[chunk(k)],
            dst_ref=band_ref.at[chunk(k % pieces)],
            send_sem=b_send.at[k],
            recv_sem=b_recv.at[k % pieces],
            device_id=(k // pieces, plane),
            device_id_type=MESH,
        )

    def keep(k):
        return pltpu.make_async_copy(
            total.at[chunk(k)], band_ref.at[chunk(k % pieces)], b_recv.at[k % pieces]
        )

    @pl.when(origin)
    def _():
        @pl.loop(0, CHUNKS)
        def _(k):
            local(k).start()

    meet(n, planes, plane, mine)
    swaps = [
        exchange(n, plane, mine, source, target, t_send.at[c], t_recv.at[c])
        for c, (source, target) in enumerate(((x_ref, x_in), (g_ref, g_in), (back, arrived_ref)))
    ]

    def begin(copy, stay):
        stay.start()

        @pl.loop(1, n)
        def _(k):
            copy(k).start()

    def finish(copy, stay):
        stay.wait()

        @pl.loop(1, n)
        def _(k):
            copy(k).wait()

    begin(*swaps[0])
    begin(*swaps[1])

    @pl.loop(0, CHUNKS)
    def _(k):
        local(k).wait()

        @pl.when(jnp.logical_not(end))
        def _():
            out(k, up, w_send).start()

        @pl.when(origin)
        def _():
            out(k, planes - 1, w_down).start()

    finish(*swaps[0])
    finish(*swaps[1])
    hidden, grad_pair = hidden_grads(weights, x_in, g_in)
    over_rows = (((0,), (0,)), ((), ()))
    for t in range(TILES):
        rows = slice(t * tile, (t + 1) * tile)
        part[rows, :pair] = (
            grad_scale
            * lax.dot_general(x_in[:, rows], grad_pair, over_rows, preferred_element_type=jnp.float32)
        ).astype(jnp.bfloat16)
        part[rows, pair:] = (
            grad_scale
            * lax.dot_general(g_in[:, rows], hidden, over_rows, preferred_element_type=jnp.float32)
        ).astype(jnp.bfloat16)

        @pl.when(end)
        def _():
            @pl.loop(t * CHUNKS // TILES, (t + 1) * CHUNKS // TILES)
            def _(k):
                hop(k, side, part).start()

    for t in range(TILES):
        rows = slice(t * tile, (t + 1) * tile)
        back[:, rows] = lax.dot_general(
            grad_pair,
            weights[rows, :pair],
            (((1,), (1,)), ((), ())),
            preferred_element_type=jnp.float32,
        ).astype(jnp.bfloat16)
    begin(*swaps[2])

    @pl.when(jnp.logical_not(jnp.logical_or(origin, end)))
    def _():
        @pl.loop(0, CHUNKS)
        def _(k):
            hop(k, 0, total).wait_recv()
            rows = chunk(k)
            total[rows, :] = (
                inbox[0, rows, :].astype(jnp.float32) + part[rows, :].astype(jnp.float32)
            ).astype(jnp.bfloat16)
            hop(k, side, total).start()

    @pl.when(origin)
    def _():
        @pl.loop(0, CHUNKS)
        def _(k):
            hop(k, 0, total).wait_recv()
            hop(k, 1, total).wait_recv()
            rows = chunk(k)
            total[rows, :] = (
                inbox[0, rows, :].astype(jnp.float32)
                + inbox[1, rows, :].astype(jnp.float32)
                + part[rows, :].astype(jnp.float32)
            ).astype(jnp.bfloat16)

            @pl.when(k // pieces != mine)
            def _():
                spread(k).start()

            @pl.when(k // pieces == mine)
            def _():
                keep(k).start()

    finish(*swaps[2])

    @pl.when(jnp.logical_not(end))
    def _():
        @pl.loop(0, CHUNKS)
        def _(k):
            out(k, up, w_send).wait_send()

    @pl.when(jnp.logical_not(origin))
    def _():
        @pl.loop(0, CHUNKS)
        def _(k):
            hop(k, side, total).wait_send()

    @pl.when(origin)
    def _():
        @pl.loop(0, CHUNKS)
        def _(k):
            out(k, planes - 1, w_down).wait_send()

            @pl.when(k // pieces != mine)
            def _():
                spread(k).wait_send()

    @pl.loop(0, pieces)
    def _(k):
        keep(k).wait()


def slot_of(route_block, capacity, experts):
    onehot = (route_block[:, None] == jnp.arange(experts, dtype=jnp.int32)[None, :]).astype(
        jnp.int32
    )
    before = jnp.cumsum(onehot, axis=0) - onehot
    position = jnp.sum(before * onehot, axis=1)
    holder = 2 * (route_block % (experts // 2)) + route_block // (experts // 2)
    return holder * capacity + position


def local(tokens, out_grad, gate_prob, routing, expert_weights):
    tok_dev, model_width = tokens.shape
    planes = lax.axis_size("expert")
    n = lax.axis_size("dp")
    capacity = 2 * tok_dev // planes
    share_rows = model_width // n
    grad_scale = float(tok_dev * n) ** (-0.5)
    width = expert_weights.shape[2]
    vmem = pl.BlockSpec(memory_space=pltpu.VMEM)
    dma = pltpu.SemaphoreType.DMA
    scaled = (gate_prob * out_grad.astype(jnp.float32)).astype(jnp.bfloat16)
    slot_index = slot_of(routing[:, 0], capacity, planes)
    dispatch_table = (
        jnp.arange(planes * capacity, dtype=jnp.int32)[:, None] == slot_index[None, :]
    ).astype(jnp.bfloat16)

    def spread_out(rows):
        spread = jnp.dot(dispatch_table, rows, preferred_element_type=jnp.float32)
        return spread.astype(jnp.bfloat16)

    send_x, send_g = spread_out(tokens), spread_out(scaled)
    band, arrived = pl.pallas_call(
        functools.partial(expert_kernel, n, planes, grad_scale),
        out_shape=(
            jax.ShapeDtypeStruct((share_rows, width), jnp.bfloat16),
            jax.ShapeDtypeStruct(send_x.shape, jnp.bfloat16),
        ),
        in_specs=[pl.BlockSpec(memory_space=pl.ANY), vmem, vmem],
        out_specs=(vmem, vmem),
        scratch_shapes=[
            pltpu.VMEM((model_width, width), jnp.bfloat16),
            pltpu.VMEM(send_x.shape, jnp.bfloat16),
            pltpu.VMEM(send_x.shape, jnp.bfloat16),
            pltpu.VMEM((model_width, width), jnp.bfloat16),
            pltpu.VMEM(send_x.shape, jnp.bfloat16),
            pltpu.VMEM((2, model_width, width), jnp.bfloat16),
            pltpu.VMEM((model_width, width), jnp.bfloat16),
            dma((CHUNKS,)),
            dma((CHUNKS,)),
            dma((CHUNKS,)),
            dma((CHUNKS,)),
            dma((2, CHUNKS)),
            dma((CHUNKS,)),
            dma((CHUNKS // n,)),
            dma((3, n)),
            dma((3, n)),
        ],
        compiler_params=pltpu.CompilerParams(
            collective_id=0, has_side_effects=True, vmem_limit_bytes=KERNEL_MIB << 20
        ),
    )(expert_weights[0], send_x, send_g)
    input_grad = lax.dot_general(
        dispatch_table,
        arrived,
        (((0,), (0,)), ((), ())),
        preferred_element_type=jnp.float32,
    ).astype(jnp.bfloat16)
    return (input_grad, band.astype(jnp.float32).reshape(1, share_rows, width))


def solution(mesh):
    both = P(("dp", "expert"), None)
    return jax.shard_map(
        local,
        mesh=mesh,
        in_specs=(both, both, both, both, P("expert", None, None)),
        out_specs=(both, P("expert", "dp", None)),
        check_vma=False,
    )
```

time: 275 us -> 240 us (0.87)
  Pallas kernels: 247 us -> 233 us
  matrix products: 14.9 us -> 3.13 us
  other arithmetic: 11.4 us -> 3.2 us
    pallas_call x2 -> x1, Pallas kernels: 247 us -> 233 us  [local(): pl.pallas_call(functools.partial(expert_kernel, n, planes, grad_scale), o...]
    dot_general x8 -> x3, matrix products: 14.9 us -> 3.13 us  [the longest x2 1.98 us: spread_out(): spread = jnp.dot(dispatch_table, rows, preferred_element_type=jnp.float32)]
    convert_element_type x1 -> x0, other arithmetic: 5.79 us -> none  [local(): weight_term(rows_in, grad_in, hidden, grad_pair, grad_scale)]
where the time goes in v3:
time: 240 us
  Pallas kernels  233 us (97%)
  other arithmetic  3.2 us (1%)
  matrix products  3.13 us (1%)
    pallas_call x1, Pallas kernels, local(): pl.pallas_call(functools.partial(expert_kernel, n, planes, grad_scale), o...  233 us

profile of v3, /device:TPU:31, one launch (start us, length us, event | category | flops | bytes accessed | tf_op | source)
XLA Modules:
  0.0 240.0 jit_solution(16702184016402922704)
XLA Ops:
  0.6 0.0 copy-start
  0.6 0.8 fusion.4
  1.4 0.2 reduce_window_sum.11
  1.6 0.8 select_reduce_fusion
  2.4 0.7 multiply_add_fusion
  3.1 1.6 convolution_convert_fusion.g_ref
  4.7 0.0 copy-done
  4.7 0.4 convolution_convert_fusion.1.x_ref
  5.1 233.0 %shard_map.68 = (bf16[64,1152]{1,0:T(8,128)(2,1)S(1)}, bf16[256,2048]{1,0:T(8,128)(2,1)S(1)}) custom-call(bf16[2048,1152]{1,0:T(8,128)(2,1)} %bitcast.9, bf16[256,2048]{1,0:T(8,128)(2,1)S(1)} %convolution_convert_fusion.1.x_ref, bf16[256,2048]{1,0:T(8,128)(2,1)S(1)} %convolution_convert_fusion.g_ref), custom_call_target="tpu_custom_call" | custom-call | tf_op jit(solution)/shard_map/pallas_call | solution.py:305
  238.1 1.1 convolution_convert_fusion.2
  239.3 0.7 bitcast_convert_fusion
Async XLA Ops:
  0.6 4.1 %copy-start = (bf16[128,2048]{1,0:T(8,128)(2,1)S(1)}, bf16[128,2048]{1,0:T(8,128)(2,1)}, u32[]{:S(2)}) copy-start(bf16[128,2048]{1,0:T(8,128)(2,1)} %param.5) | copy-start | bytes 1572868

commit v4 on v3

--- a/solution.py
+++ b/solution.py
@@ -164,11 +164,7 @@
         def _(k):
             copy(k).wait()
 
-    begin(*swaps[0])
-    begin(*swaps[1])
-
-    @pl.loop(0, CHUNKS)
-    def _(k):
+    def pass_on(k):
         local(k).wait()
 
         @pl.when(jnp.logical_not(end))
@@ -179,6 +175,11 @@
         def _():
             out(k, planes - 1, w_down).start()
 
+    ahead = jnp.where(origin, CHUNKS // 4, 0)
+    pl.loop(0, ahead)(pass_on)
+    begin(*swaps[0])
+    begin(*swaps[1])
+    pl.loop(ahead, CHUNKS)(pass_on)
     finish(*swaps[0])
     finish(*swaps[1])
     hidden, grad_pair = hidden_grads(weights, x_in, g_in)
@@ -272,11 +273,10 @@
 
 
 def slot_of(route_block, capacity, experts):
-    onehot = (route_block[:, None] == jnp.arange(experts, dtype=jnp.int32)[None, :]).astype(
-        jnp.int32
-    )
-    before = jnp.cumsum(onehot, axis=0) - onehot
-    position = jnp.sum(before * onehot, axis=1)
+    order = jnp.arange(route_block.shape[0], dtype=jnp.int32)
+    same = route_block[:, None] == route_block[None, :]
+    earlier = order[None, :] < order[:, None]
+    position = jnp.sum(jnp.logical_and(same, earlier).astype(jnp.int32), axis=1)
     holder = 2 * (route_block % (experts // 2)) + route_block // (experts // 2)
     return holder * capacity + position
 

time: 240 us -> 238 us (level)
  no operation moved by 1% of the time
where the time goes in v4:
time: 238 us
  Pallas kernels  232 us (97%)
  matrix products  3.13 us (1%)
    pallas_call x1, Pallas kernels, local(): pl.pallas_call(functools.partial(expert_kernel, n, planes, grad_scale), o...  232 us

profile of v4, /device:TPU:31, one launch (start us, length us, event | category | flops | bytes accessed | tf_op | source)
XLA Modules:
  0.0 238.1 jit_solution(17453805939020343074)
XLA Ops:
  0.6 0.0 copy-start
  0.6 0.9 convert_reduce_fusion
  1.5 0.7 multiply_add_fusion
  2.2 1.6 convolution_convert_fusion.g_ref
  3.8 0.0 copy-done
  3.8 0.4 convolution_convert_fusion.1.x_ref
  4.2 232.0 %shard_map.68 = (bf16[64,1152]{1,0:T(8,128)(2,1)S(1)}, bf16[256,2048]{1,0:T(8,128)(2,1)S(1)}) custom-call(bf16[2048,1152]{1,0:T(8,128)(2,1)} %bitcast.9, bf16[256,2048]{1,0:T(8,128)(2,1)S(1)} %convolution_convert_fusion.1.x_ref, bf16[256,2048]{1,0:T(8,128)(2,1)S(1)} %convolution_convert_fusion.g_ref), custom_call_target="tpu_custom_call" | custom-call | tf_op jit(solution)/shard_map/pallas_call | solution.py:305
  236.2 1.1 convolution_convert_fusion.2
  237.4 0.7 bitcast_convert_fusion
Async XLA Ops:
  0.6 3.2 %copy-start = (bf16[128,2048]{1,0:T(8,128)(2,1)S(1)}, bf16[128,2048]{1,0:T(8,128)(2,1)}, u32[]{:S(2)}) copy-start(bf16[128,2048]{1,0:T(8,128)(2,1)} %param.5) | copy-start | bytes 1572868
